TPU v7x, 32 devices: a whole 2x2x4 slice. The times are simulated.
32 devices in a mesh: tm: 16 (over z, y, x), rep: 2 (over core).
Axes of the slice: x: 2, y: 2, z: 4, core: 2. Of those that a mesh axis runs over, the one named last changes fastest.
Arguments:
- rows: float32 [65536, 256], P('tm', 'rep'), may hold values from -90 to 90, as said below
- row_mask: int32 [65536], P('tm'), may hold values from 0 to 1, as said below
- key_bucket: int32 [65536], P('tm'), may hold values from 0 to 15
- gain: float32 [256], P('rep'), may hold values from 0.1 to 1.9
Outputs:
- keyed: float32 [49152, 256], P('tm', 'rep')
Inputs may be any that keep to these rules, and one draw needn't show every extreme that they name: `rows`: scale per column differs; entries stay in the range. `row_mask`: of the 4096 rows of each index of tm, at least 2048 pass. Among the passing rows of one index of tm, no key bucket occurs more than 192 times, and one bucket, the same for all indices, occurs exactly 192 times on every index.
All inputs are finite; a program needn't handle non-finite values.
Results may differ from a plain program's by a relative error of at most 0.0003.
Values sent between devices are 32-bit elements; how exact they have to be, the bound alone decides.
A program may use at most 64 MiB of HBM per device.

v0:
```python
import jax
import jax.numpy as jnp
from jax import lax
from jax.sharding import PartitionSpec as P

F = 256
WINDOW = 512


epsilon = 1e-06


def passed_along(x, axis, by):
    devices = lax.axis_size(axis)
    return lax.ppermute(x, axis, [(i, (i + by) % devices) for i in range(devices)])


def window_sums(extended, width):
    blocks = extended.reshape(-1, width, extended.shape[1])
    steps = jnp.arange(width, dtype=jnp.int32)
    lower = (steps[:, None] >= steps[None, :]).astype(jnp.float32)
    inner = jnp.einsum("ij,bjf->bif", lower, blocks, precision=lax.Precision.HIGHEST)
    totals = inner[:, -1:, :]
    result = inner[1:] + totals[:-1] - inner[:-1]
    return result.reshape(-1, extended.shape[1])


def bucket_ranks(hits):
    size_rows, buckets = hits.shape
    block = min(512, size_rows)
    grouped = hits.reshape(size_rows // block, block, buckets)
    steps = jnp.arange(block, dtype=jnp.int32)
    lower = (steps[:, None] >= steps[None, :]).astype(jnp.float32)
    within = jnp.einsum("ij,bjc->bic", lower, grouped, precision=lax.Precision.HIGHEST)
    totals = within[:, -1, :]
    earlier = jnp.cumsum(totals, axis=0) - totals
    running = (within + earlier[:, None, :]).reshape(size_rows, buckets)
    local_rank = (jnp.sum(running * hits, axis=1) - 1.0).astype(jnp.int32)
    counts = jnp.sum(totals, axis=0).astype(jnp.int32)
    return (local_rank, counts)


def compact_rows(payload, row_mask):
    size_rows, width = payload.shape
    live = row_mask == 1
    order_rank = jnp.cumsum(row_mask) - 1
    target = jnp.where(live, order_rank, size_rows)
    return jnp.zeros((size_rows, width), jnp.float32).at[target].set(payload, mode="drop")


def fill_slots(values, slot, slots_total):
    width = values.shape[1]
    return jnp.zeros((slots_total, width), jnp.float32).at[slot].set(values, mode="drop")


def local(rows, row_mask, key_bucket, gain):
    size_rows, half = rows.shape
    nodes = lax.axis_size("tm")
    most = 3 * size_rows // (4 * nodes)
    positions = jnp.arange(size_rows, dtype=jnp.int32)
    bucket_ids = jnp.arange(nodes, dtype=jnp.int32)
    count = jnp.sum(row_mask)
    own_hits = (key_bucket[:, None] == bucket_ids[None, :]).astype(jnp.float32)
    payload = jnp.concatenate([rows, own_hits], axis=1)
    packed = compact_rows(payload, row_mask)
    compact = packed[:, :half]
    hits = packed[:, half:]
    valid = positions < count
    key_value = jnp.dot(
        hits,
        bucket_ids.astype(jnp.float32),
        precision=lax.Precision.HIGHEST,
        preferred_element_type=jnp.float32,
    )
    compact_key = jnp.where(valid, key_value.astype(jnp.int32), nodes)
    tail = lax.dynamic_slice_in_dim(compact, count - WINDOW, WINDOW, 0)
    earlier_tail = passed_along(tail, "tm", 1)
    extended = jnp.concatenate([earlier_tail, compact], axis=0)
    sums = window_sums(extended, WINDOW)
    squares = jnp.sum(sums * sums, axis=1)
    full = lax.psum(squares, "rep")
    values = sums * gain[None, :] / jnp.sqrt(full[:, None] / F + epsilon)
    local_rank, counts = bucket_ranks(hits)
    slot = jnp.where(valid, compact_key * most + local_rank, nodes * most)
    outgoing = fill_slots(values, slot, nodes * most)
    outgoing = outgoing.reshape(nodes, most * half)
    sideband = counts.astype(jnp.float32)[:, None]
    received, got_side = (
        lax.all_to_all(outgoing, "tm", split_axis=0, concat_axis=0, tiled=True),
        lax.all_to_all(sideband, "tm", split_axis=0, concat_axis=0, tiled=True),
    )
    got_numbers = got_side.astype(jnp.int32)
    got_starts = jnp.cumsum(got_numbers, axis=0) - got_numbers
    capacity = nodes * most
    start_list = got_starts.reshape(-1)
    spots = jnp.arange(capacity, dtype=jnp.int32)
    sender = jnp.sum((start_list[None, :] <= spots[:, None]).astype(jnp.int32), axis=1) - 1
    sender = jnp.maximum(sender, 0)
    offset = spots - start_list[sender]
    inside = (offset >= 0) & (offset < most)
    lookup = sender * most + jnp.clip(offset, 0, most - 1)
    flat = received.reshape(-1, half)
    keyed = jnp.where(inside[:, None], flat[lookup], jnp.float32(0.0))
    return keyed


def solution(mesh):
    in_specs = (P("tm", "rep"), P("tm"), P("tm"), P("rep"))
    out_specs = P("tm", "rep")
    return jax.shard_map(local, mesh=mesh, in_specs=in_specs, out_specs=out_specs, check_vma=False)
```

profile of v0, /device:TPU:15, one launch (start us, length us, event | category | flops | bytes accessed | tf_op | source)
XLA Modules:
  0.0 127.6 jit_solution(7532041285759532426)
XLA Ops:
  0.0 1.0 reduce-window.14
  1.2 1.4 %fusion.20 = (s32[]{:T(128)}, s32[4096]{0:T(1024)S(1)}) fusion(s32[4096]{0:T(1024)} %param.5, s32[32,128]{1,0:T(8,128)S(1)} %reduce-window.14, s32[32]{0:T(128)S(1)} %slice_reduce_fusion.2), kind=kLoop, calls=%fused_computation.53 | loop fusion | flops 32767 | bytes 49284 | tf_op jit(solution)/shard_map/reduce_sum | solution.py:62
  2.7 1.3 %fusion.7 = f32[4096,16]{1,0:T(8,128)S(1)} fusion(s32[4096]{0:T(1024)} %param.6), kind=kLoop, calls=%fused_computation.17 | loop fusion | flops 131072 | bytes 278528 | tf_op jit(solution)/shard_map/convert_element_type | solution.py:63
  4.0 20.2 %scatter_custom_fusion = f32[4096,144]{1,0:T(8,128)} fusion(s32[4096]{0:T(1024)S(1)} %get-tuple-element.10, f32[4096,16]{1,0:T(8,128)S(1)} %fusion.7, f32[]{:T(128)} %constant.74, f32[4096,128]{1,0:T(8,128)} %param.4, f32[]{:T(128)} %constant.14.clone.1), kind=kCustom, calls=%fused_computation.3 | custom fusion | flops 589824 | bytes 6553608 | tf_op jit(solution)/shard_map/scatter | solution.py:48
  24.2 1.7 %slice.58 = f32[4096,128]{1,0:T(8,128)S(1)} slice(f32[4096,144]{1,0:T(8,128)} %scatter_custom_fusion), slice={[0:4096], [0:128]} | slice | bytes 4194304 | tf_op jit(solution)/shard_map/slice | solution.py:66
  27.3 1.3 collective-permute-start
  28.6 0.3 slice-done
  28.9 3.4 %convolution_bitcast_fusion.1 = f32[8,512,16]{1,2,0:T(8,128)S(1)} fusion(f32[8,512,16]{2,1,0:T(8,128)S(1)} %bitcast.56), kind=kOutput, calls=%fused_computation.19 | convolution fusion | flops 402915328 | bytes 524288 | tf_op jit(solution)/shard_map/ij,bjc->bic/dot_general | solution.py:34
  32.3 0.2 slice_reduce_fusion.1
  32.5 0.7 copy.33
  33.2 6.6 %all-to-all-start = ((f32[16,1,1]{2,1,0:T(1,128)}), f32[16,1,1]{2,1,0:T(1,128)S(1)}, u32[]{:S(2)}, u32[]{:S(2)}) async-start(f32[16,1,1]{2,1,0:T(1,128)} %copy.33), calls=%async_computation | async-start | bytes 16384 | tf_op jit(solution)/shard_map/all_to_all | solution.py:90
  39.8 0.2 fusion.22
  40.0 3.5 %fusion.15 = f32[1,4096]{1,0:T(1,128)S(1)} fusion(f32[4096,144]{1,0:T(8,128)} %scatter_custom_fusion), kind=kOutput, calls=%fused_computation.45 | convolution fusion | flops 786448 | bytes 2113536 | tf_op jit(solution)/shard_map/dot_general | solution.py:69
  43.6 0.6 copy.43
  44.2 2.6 %fusion.5 = f32[4096]{0:T(1024)S(1)} fusion(f32[8,512,16]{2,1,0:T(8,128)S(1)} %copy.43, f32[4096,144]{1,0:T(8,128)} %scatter_custom_fusion), kind=kLoop, calls=%fused_computation.13 | loop fusion | flops 126976 | bytes 540672 | tf_op jit(solution)/shard_map/reduce_sum | solution.py:38
  46.8 0.7 compare_select_fusion.1
  47.4 0.2 pad_maximum_fusion
  47.6 3.9 %convolution_bitcast_fusion = f32[9,512,128]{1,2,0:T(8,128)S(1)} fusion(f32[9,512,128]{2,1,0:T(8,128)S(1)} %bitcast.57), kind=kOutput, calls=%fused_computation.18 | convolution fusion | flops 3624140800 | bytes 4718592 | tf_op jit(solution)/shard_map/ij,bjf->bif/dot_general | solution.py:22
  51.5 0.4 slice_reduce_fusion
  51.9 1.8 %multiply_reduce_fusion = (f32[8,512]{1,0:T(8,128)S(1)}, f32[8,512,128]{1,2,0:T(8,128)}) fusion(f32[9,512,128]{1,2,0:T(8,128)S(1)} %convolution_bitcast_fusion, f32[8,128]{1,0:T(8,128)S(1)} %slice_reduce_fusion), kind=kLoop, calls=%fused_computation.14 | loop fusion | flops 2093056 | bytes 6311936 | tf_op jit(solution)/shard_map/reduce_sum | solution.py:80
  53.7 1.9 %copy.38 = f32[8,512,128]{2,1,0:T(8,128)S(1)} copy(f32[8,512,128]{1,2,0:T(8,128)} %get-tuple-element.8) | data formatting | bytes 4194304 | tf_op jit(solution)/shard_map/sub | solution.py:24
  55.6 4.4 %psum.7 = f32[4096]{0:T(1024)S(1)} all-reduce(f32[4096]{0:T(1024)S(1)} %bitcast.61), channel_id=1, replica_groups=mesh['tm'=16,'rep'=2] {'rep'}, use_global_device_ids=true, to_apply=%region_10.11 | all-reduce | flops 4096 | bytes 32768 | tf_op jit(solution)/shard_map/psum | solution.py:81
  60.0 1.9 %fusion.4 = f32[4096,128]{1,0:T(8,128)} fusion(f32[8,512,128]{2,1,0:T(8,128)S(1)} %copy.38, f32[4096]{0:T(1024)S(1)} %add_sqrt_fusion, f32[128]{0:T(128)S(1)} %copy-done.2), kind=kLoop, calls=%fused_computation.11 | loop fusion | flops 1048576 | bytes 4211200 | tf_op jit(solution)/shard_map/div | solution.py:82
  61.9 12.1 %scatter_custom_fusion.1 = f32[3072,128]{1,0:T(8,128)} fusion(s32[4096]{0:T(1024)S(1)} %compare_select_fusion.1, f32[4096,128]{1,0:T(8,128)} %fusion.4, f32[]{:T(128)} %constant.14.clone.1), kind=kCustom, calls=%fused_computation.24 | custom fusion | bytes 1573376 | tf_op jit(solution)/shard_map/scatter | solution.py:53
  74.1 6.4 %all-to-all-start.1 = ((f32[16,1,24576]{2,1,0:T(1,128)}), f32[16,1,24576]{2,1,0:T(1,128)S(1)}, u32[]{:S(2)}, u32[]{:S(2)}) async-start(f32[16,1,24576]{2,1,0:T(1,128)} %bitcast.29), calls=%async_computation.1 | async-start | bytes 3145728 | tf_op jit(solution)/shard_map/all_to_all | solution.py:89
  80.5 0.1 reduce.3
  80.6 0.4 convert_reduce_fusion.1
  81.0 0.7 fusion.21
  81.8 9.9 %compare_and_fusion = (pred[3072]{0:T(1024)(128)(4,1)S(1)}, s32[3072]{0:T(1024)S(1)}) fusion(s32[]{:T(128)} %bitcast.22, s32[]{:T(128)} %bitcast.21, s32[]{:T(128)} %bitcast.20, s32[]{:T(128)} %bitcast.19, s32[]{:T(128)} %bitcast.18, s32[]{:T(128)} %bitcast.17, s32[]{:T(128)} %bitcast.16, s32[]{:T(128)} %bitcast.15, s32[]{:T(128)} %bitcast.14, s32[]{:T(128)} %bitcast.13, ...), kind=kLoop, calls=%fused_computation.42 | loop fusion | flops 110592 | bytes 27712 | tf_op jit(solution)/shard_map/and | solution.py:100
  91.8 25.2 %all-to-all-done.1 = f32[16,1,24576]{2,1,0:T(1,128)S(1)} async-done(((f32[16,1,24576]{2,1,0:T(1,128)}), f32[16,1,24576]{2,1,0:T(1,128)S(1)}, u32[]{:S(2)}, u32[]{:S(2)}) %all-to-all-start.1) | async-done | bytes 1572896 | tf_op jit(solution)/shard_map/all_to_all | solution.py:89
  117.0 8.1 %gather_fusion = f32[3072,128]{1,0:T(8,128)S(1)} fusion(f32[3072,128]{1,0:T(8,128)S(1)} %bitcast.55, s32[3072]{0:T(1024)S(1)} %broadcast_clamp_fusion), kind=kCustom, calls=%fused_computation | custom fusion | bytes 3158016 | tf_op jit(solution)/shard_map/gather | solution.py:103
  125.1 2.5 %broadcast_select_fusion = f32[3072,128]{1,0:T(8,128)} fusion(f32[3072,128]{1,0:T(8,128)S(1)} %gather_fusion, pred[3072]{0:T(1024)(128)(4,1)S(1)} %get-tuple-element.5), kind=kLoop, calls=%fused_computation.23 | loop fusion | flops 393216 | bytes 3148800 | tf_op jit(solution)/shard_map/jit(_where)/select_n | solution.py:103
  (24 shorter events, 0.6 us)
Async XLA Ops:
  25.9 1.4 %copy-start = (f32[4096,128]{1,0:T(8,128)}, f32[4096,128]{1,0:T(8,128)S(1)}, u32[]{:S(2)}) copy-start(f32[4096,128]{1,0:T(8,128)S(1)} %slice.58) | copy-start | bytes 6291460
  27.3 1.6 %slice-start = ((f32[4096,144]{1,0:T(8,128)}), f32[4096,16]{1,0:T(8,128)S(1)}, s32[]{:S(2)}) async-start(f32[4096,144]{1,0:T(8,128)} %scatter_custom_fusion), calls=%async_computation.2 | async-start | bytes 4194304 | tf_op jit(solution)/shard_map/slice | solution.py:67
  27.3 20.1 %collective-permute-start = (f32[512,128]{1,0:T(8,128)S(1)}, f32[512,128]{1,0:T(8,128)S(1)}, u32[]{:S(2)}, u32[]{:S(2)}) collective-permute-start(f32[512,128]{1,0:T(8,128)S(1)} %constant_dynamic-slice_fusion), channel_id=1, source_target_pairs={{0,2},{2,4},{4,6},{6,8},{8,10},{10,12},{12,14},{14,16},{16,18},{18... | collective-permute-start | bytes 786440 | tf_op jit(solution)/shard_map/ppermute | solution.py:15
  33.2 40.9 %all-to-all-start = ((f32[16,1,1]{2,1,0:T(1,128)}), f32[16,1,1]{2,1,0:T(1,128)S(1)}, u32[]{:S(2)}, u32[]{:S(2)}) async-start(f32[16,1,1]{2,1,0:T(1,128)} %copy.33), calls=%async_computation | async-start | bytes 16384 | tf_op jit(solution)/shard_map/all_to_all | solution.py:90
  44.2 3.3 %copy-start.1 = (f32[4096,128]{1,0:T(8,128)S(1)}, f32[4096,128]{1,0:T(8,128)}, u32[]{:S(2)}) copy-start(f32[4096,128]{1,0:T(8,128)} %copy-done) | copy-start | bytes 6291460
  53.7 6.4 %copy-start.2 = (f32[128]{0:T(128)S(1)}, f32[128]{0:T(128)}, u32[]{:S(2)}) copy-start(f32[128]{0:T(128)} %param.7) | copy-start | bytes 1540
  74.1 42.9 %all-to-all-start.1 = ((f32[16,1,24576]{2,1,0:T(1,128)}), f32[16,1,24576]{2,1,0:T(1,128)S(1)}, u32[]{:S(2)}, u32[]{:S(2)}) async-start(f32[16,1,24576]{2,1,0:T(1,128)} %bitcast.29), calls=%async_computation.1 | async-start | bytes 3145728 | tf_op jit(solution)/shard_map/all_to_all | solution.py:89
where the time goes:
time: 129 us; the launch traced here: 128 us
  other arithmetic  44.6 us (35%)
  local copies, waits for them, and re-layouts  26.8 us (21%)
  waiting for transfers between devices  25.2 us (20%)
  starting transfers between devices  14.2 us (11%)
  matrix products  10.8 us (8%)
  blocking collectives  4.43 us (3%)
  between operations  1.56 us (1%)
    all_to_all x1, waiting for transfers between devices, local(): lax.all_to_all(outgoing, 'tm', split_axis=0, concat_axis=0, tiled=True)  25.2 us
    scatter x1, other arithmetic, compact_rows(): jnp.zeros((size_rows, width), jnp.float32).at[target]  20.2 us
    scatter x1, local copies, waits for them, and re-layouts, fill_slots(): jnp.zeros((slots_total, width), jnp.float32).at[slot]  12.1 us
    and x1, other arithmetic, local(): inside = (offset >= 0) & (offset < most)  9.94 us
    gather x1, local copies, waits for them, and re-layouts, local(): keyed = jnp.where(inside[:, None], flat[lookup], jnp.float32(0.0))  8.11 us
    all_to_all x1, starting transfers between devices, local(): lax.all_to_all(sideband, 'tm', split_axis=0, concat_axis=0, tiled=True)  6.58 us
    all_to_all x1, starting transfers between devices, local(): lax.all_to_all(outgoing, 'tm', split_axis=0, concat_axis=0, tiled=True)  6.36 us
    psum x1, blocking collectives, local(): full = lax.psum(squares, 'rep')  4.43 us
  transfers between devices with their start and end apart: 3, of which 1 were waited for; matrix products, arithmetic and copies ran while one was open for 36% of the time, Pallas kernels for 0%

commit v1 on v0

v1 whole, which is shorter than its diff:
```python
import functools

import jax
import jax.numpy as jnp
from jax import lax
from jax.experimental import pallas as pl
from jax.experimental.pallas import tpu as pltpu
from jax.sharding import PartitionSpec as P

F = 256
WINDOW = 512
EPS = 1e-06
LANES = 128
STEP = 64
VMEM = pltpu.MemorySpace.VMEM
SMEM = pltpu.MemorySpace.SMEM
f32, bf16, i32 = jnp.float32, jnp.bfloat16, jnp.int32


def iota(shape, axis):
    return lax.broadcasted_iota(i32, shape, axis)


def dot(a, b):
    return jnp.dot(a, b, preferred_element_type=f32)


def compact_kernel(nodes, most, rows, mask, key, empty, packed, tail, source, counts,
                   place_v, slot_v, place_s, slot_s, sems):
    lines = mask.shape[0]
    slots = nodes * most
    fill = pltpu.make_async_copy(empty, source, sems.at[0])
    fill.start()
    one = jnp.ones((), f32)
    upper = (iota((LANES, LANES), 0) <= iota((LANES, LANES), 1)).astype(f32).astype(bf16)
    both = jnp.concatenate([upper, jnp.ones((LANES, LANES), bf16)], axis=0)
    group = min(nodes, 16)
    size = group * lines
    r, c = iota((size, size), 0), iota((size, size), 1)
    earlier = ((r // lines == c // lines) & (c < r)).astype(f32).astype(bf16)

    live = mask[...] == 1
    livef = live.astype(f32)
    keys = key[...]

    def prefix(hits, lower):
        hits = hits.astype(bf16)
        above = dot(lower, hits).astype(bf16)
        return dot(jnp.concatenate([hits, above], axis=1), both)

    place_v[...] = (prefix(livef, earlier[:lines, :lines]) - livef).astype(i32)
    slot = (one - livef) * slots
    lane = iota((8, LANES), 1)
    parts = []
    for first in range(0, nodes, group):
        hits = [(live & (keys == b)).astype(f32) for b in range(first, first + group)]
        running = prefix(jnp.concatenate(hits, axis=0), earlier)
        for j, hit in enumerate(hits):
            b = first + j
            mine = running[j * lines:(j + 1) * lines]
            slot = slot + hit * (mine + (b * most - 1.0))
            parts.append(jnp.where(lane == b % LANES, mine[lines - 1:lines, LANES - 1:LANES], 0.0))
    counts[...] = sum(parts)
    slot_v[...] = slot.astype(i32)
    c1 = pltpu.make_async_copy(place_v, place_s, sems.at[1])
    c2 = pltpu.make_async_copy(slot_v, slot_s, sems.at[2])
    c1.start()
    c2.start()
    fill.wait()
    c1.wait()
    c2.wait()

    def line(i, carry):
        def some(q, carry):
            for u in range(16):
                j = q * 16 + u
                g = place_s[i, j]
                packed[pl.ds(g, 1), :] = rows[pl.ds(i * LANES + j, 1), :]
                source[slot_s[i, j]] = g
            return carry
        return lax.fori_loop(0, LANES // 16, some, carry)

    lax.fori_loop(0, lines, line, 0)
    count = place_s[lines - 1, LANES - 1] + (slot_s[lines - 1, LANES - 1] < slots).astype(i32)
    tail[...] = packed[pl.ds(count - WINDOW, WINDOW), :]


def exchange_kernel(nodes, most, packed, tail, source, counts, gain, got, gotc,
                    tailbuf, w8, w64, sums, mine, other, send,
                    tsem, qsem, ssem, rsem, cssem, crsem):
    slots = nodes * most
    me, rep = lax.axis_index("tm"), lax.axis_index("rep")
    barrier = pltpu.get_barrier_semaphore()

    def hello(k, carry):
        pl.semaphore_signal(barrier, inc=1, device_id={"tm": lax.rem(me + k, nodes)})
        return carry

    lax.fori_loop(1, nodes, hello, 0)
    pl.semaphore_signal(barrier, inc=1, device_id={"rep": 1 - rep})
    pl.semaphore_wait(barrier, nodes)

    ahead = pltpu.make_async_remote_copy(
        src_ref=tail, dst_ref=tailbuf, send_sem=tsem.at[0], recv_sem=tsem.at[1],
        device_id={"tm": lax.rem(me + 1, nodes)})
    ahead.start()

    def count_copy(d, at):
        return pltpu.make_async_remote_copy(
            src_ref=counts, dst_ref=gotc.at[at], send_sem=cssem.at[d], recv_sem=crsem.at[at],
            device_id={"tm": d})

    def send_counts(k, carry):
        count_copy(lax.rem(me + k, nodes), me).start()
        return carry

    lax.fori_loop(1, nodes, send_counts, 0)
    gotc[me] = counts[...]

    def eight(x):
        x = x + pltpu.roll(x, 1, 0)
        x = x + pltpu.roll(x, 2, 0)
        x = x + pltpu.roll(x, 4, 0)
        return x[8:]

    def w8_own(c, carry):
        a = pl.multiple_of(c * STEP, STEP)
        w8[pl.ds(WINDOW + a, STEP), :] = eight(packed[pl.ds(a - 8, STEP + 8), :])
        return carry

    def stride_sum(ref, a, rows, stride):
        parts = [ref[pl.ds(a - stride * k, rows), :] for k in range(8)]
        while len(parts) > 1:
            parts = [parts[i] + parts[i + 1] for i in range(0, len(parts), 2)]
        return parts[0]

    def w64_at(c, carry):
        a = pl.multiple_of(c * STEP, STEP)
        w64[pl.ds(a, STEP), :] = stride_sum(w8, a, STEP, 8)
        return carry

    ones = jnp.ones((8, LANES), f32)

    def w512_at(c, carry):
        a = pl.multiple_of(c * LANES, LANES)
        total = stride_sum(w64, WINDOW + a, LANES, 64)
        sums[pl.ds(a, LANES), :] = total
        sq = lax.dot_general(ones, total * total, (((1,), (1,)), ((), ())),
                             precision=lax.Precision.HIGHEST, preferred_element_type=f32)
        mine[pl.ds(c, 1), :] = sq[0:1]
        return carry

    own = WINDOW // STEP + 1
    last = (WINDOW + slots) // STEP
    lax.fori_loop(1, slots // STEP, w8_own, 0)
    lax.fori_loop(own + 1, last, w64_at, 0)
    lax.fori_loop(5, slots // LANES, w512_at, 0)
    ahead.wait()
    w8[0:STEP, :] = eight(jnp.concatenate([jnp.zeros((8, LANES), f32), tailbuf[0:STEP, :]], axis=0))
    for a in range(STEP, WINDOW, STEP):
        w8[a:a + STEP, :] = eight(tailbuf[a - 8:a + STEP, :])
    w8[WINDOW:WINDOW + STEP, :] = eight(
        jnp.concatenate([tailbuf[WINDOW - 8:WINDOW, :], packed[0:STEP, :]], axis=0))
    lax.fori_loop(1, own + 1, w64_at, 0)
    lax.fori_loop(0, 5, w512_at, 0)

    swap = pltpu.make_async_remote_copy(
        src_ref=mine, dst_ref=other, send_sem=qsem.at[0], recv_sem=qsem.at[1],
        device_id={"rep": 1 - rep})
    swap.start()
    sums[pl.ds(slots, 8), :] = jnp.zeros((8, LANES), f32)
    swap.wait()

    gains = gain[...]

    def scale(c, carry):
        a = pl.multiple_of(c * LANES, LANES)
        full = mine[pl.ds(c, 1), :] + other[pl.ds(c, 1), :]
        inv = lax.rsqrt(full / F + EPS)
        column = jnp.broadcast_to(inv, (LANES, LANES)).T
        sums[pl.ds(a, LANES), :] = sums[pl.ds(a, LANES), :] * gains * column
        return carry

    lax.fori_loop(0, slots // LANES, scale, 0)

    def gather(ref, d):
        def some(q, carry):
            for u in range(8):
                j = q * 8 + u
                ref[d, pl.ds(j, 1), :] = sums[pl.ds(source[d * most + j], 1), :]
            return carry
        lax.fori_loop(0, most // 8, some, 0)

    def block_copy(d, at):
        return pltpu.make_async_remote_copy(
            src_ref=send.at[d], dst_ref=got.at[at], send_sem=ssem.at[d], recv_sem=rsem.at[at],
            device_id={"tm": d})

    def send_block(k, carry):
        d = lax.rem(me + k, nodes)
        gather(send, d)
        block_copy(d, me).start()
        return carry

    lax.fori_loop(1, nodes, send_block, 0)
    gather(got, me)

    def finish(k, carry):
        s = lax.rem(me + k, nodes)
        count_copy(s, s).wait()
        block_copy(s, s).wait()
        return carry

    lax.fori_loop(1, nodes, finish, 0)


def place_kernel(nodes, most, got, gotc, out):
    me = lax.axis_index("tm")
    out[...] = jnp.zeros_like(out)
    lane = iota((1, LANES), 1)

    def sender(s, start):
        out[pl.ds(start, most), :] = got[s]
        number = jnp.sum(jnp.where(lane == me, gotc[s, 0:1, :], 0.0))
        return start + number.astype(i32)

    lax.fori_loop(0, nodes, sender, jnp.int32(0))


def local(nodes, rows, row_mask, key_bucket, gain):
    size_rows, half = rows.shape
    most = 3 * size_rows // (4 * nodes)
    slots = nodes * most
    lines = size_rows // LANES
    vm = pl.BlockSpec(memory_space=VMEM)
    sm = pl.BlockSpec(memory_space=SMEM)
    hbm = pl.BlockSpec(memory_space=pl.ANY)
    empty = jnp.full((slots + LANES,), slots, i32)
    packed, tail, source, counts = pl.pallas_call(
        functools.partial(compact_kernel, nodes, most),
        out_shape=(
            jax.ShapeDtypeStruct((slots + 8, half), f32),
            jax.ShapeDtypeStruct((WINDOW, half), f32),
            jax.ShapeDtypeStruct((slots + LANES,), i32),
            jax.ShapeDtypeStruct((8, LANES), f32),
        ),
        in_specs=[vm, vm, vm, hbm],
        out_specs=(vm, vm, sm, vm),
        scratch_shapes=[
            pltpu.VMEM((lines, LANES), i32),
            pltpu.VMEM((lines, LANES), i32),
            pltpu.SMEM((lines, LANES), i32),
            pltpu.SMEM((lines, LANES), i32),
            pltpu.SemaphoreType.DMA((3,)),
        ],
        name="compact",
    )(rows, row_mask.reshape(lines, LANES), key_bucket.reshape(lines, LANES), empty)
    dma = pltpu.SemaphoreType.DMA
    got, gotc = pl.pallas_call(
        functools.partial(exchange_kernel, nodes, most),
        out_shape=(
            jax.ShapeDtypeStruct((nodes, most, half), f32),
            jax.ShapeDtypeStruct((nodes, 8, LANES), f32),
        ),
        in_specs=[vm, vm, sm, vm, vm],
        out_specs=(vm, vm),
        scratch_shapes=[
            pltpu.VMEM((WINDOW, half), f32),
            pltpu.VMEM((WINDOW + slots, half), f32),
            pltpu.VMEM((WINDOW + slots, half), f32),
            pltpu.VMEM((slots + 8, half), f32),
            pltpu.VMEM((slots // LANES, LANES), f32),
            pltpu.VMEM((slots // LANES, LANES), f32),
            pltpu.VMEM((nodes, most, half), f32),
            dma((2,)), dma((2,)), dma((nodes,)), dma((nodes,)), dma((nodes,)), dma((nodes,)),
        ],
        compiler_params=pltpu.CompilerParams(collective_id=0, has_side_effects=True),
        name="exchange",
    )(packed, tail, source, counts, gain.reshape(1, half))
    return pl.pallas_call(
        functools.partial(place_kernel, nodes, most),
        out_shape=jax.ShapeDtypeStruct((slots, half), f32),
        in_specs=[vm, vm],
        out_specs=vm,
        name="place",
    )(got, gotc)


def solution(mesh):
    in_specs = (P("tm", "rep"), P("tm"), P("tm"), P("rep"))
    body = functools.partial(local, mesh.shape["tm"])
    return jax.shard_map(body, mesh=mesh, in_specs=in_specs, out_specs=P("tm", "rep"), check_vma=False)
```

time: 129 us -> 82.3 us (0.64)
  Pallas kernels: 0 us -> 81.5 us
  other arithmetic: 44.6 us -> 0 us
  local copies, waits for them, and re-layouts: 26.8 us -> 0.6 us
  waiting for transfers between devices: 25.2 us -> 0 us
  starting transfers between devices: 14.2 us -> 0 us
  matrix products: 10.8 us -> 0 us
  blocking collectives: 4.43 us -> 0 us
  between operations: 1.56 us -> 0.02 us
    pallas_call x0 -> x3, Pallas kernels: none -> 81.5 us  [the longest x1 59.9 us: local(): pl.pallas_call(functools.partial(exchange_kernel, nodes, most), out_shape...]
    all_to_all x2 -> x0, waiting for transfers between devices: 25.2 us -> none  [the longest x1 25.2 us: local(): lax.all_to_all(outgoing, 'tm', split_axis=0, concat_axis=0, tiled=True)]
    scatter x1 -> x0, other arithmetic: 20.2 us -> none  [compact_rows(): jnp.zeros((size_rows, width), jnp.float32).at[target]]
    all_to_all x2 -> x0, starting transfers between devices: 12.9 us -> none  [the longest x1 6.58 us: local(): lax.all_to_all(sideband, 'tm', split_axis=0, concat_axis=0, tiled=True)]
    scatter x1 -> x0, local copies, waits for them, and re-layouts: 12.1 us -> none  [fill_slots(): jnp.zeros((slots_total, width), jnp.float32).at[slot]]
    dot_general x3 -> x0, matrix products: 10.8 us -> none  [the longest x1 3.91 us: window_sums(): jnp.einsum('ij,bjf->bif', lower, blocks, precision=lax.Precision.HIGHEST)]
    and x1 -> x0, other arithmetic: 9.94 us -> none  [local(): inside = (offset >= 0) & (offset < most)]
    gather x2 -> x0, local copies, waits for them, and re-layouts: 8.83 us -> none  [the longest x1 8.11 us: local(): keyed = jnp.where(inside[:, None], flat[lookup], jnp.float32(0.0))]
  transfers between devices with their start and end apart: 3 -> 0, of which waited for: 1 -> 0; matrix products, arithmetic and copies ran while one was open for 36% -> 0% of each run, Pallas kernels for 0% -> 0%
where the time goes in v1:
time: 82.3 us; the launch traced here: 82.1 us
  Pallas kernels  81.5 us (99%)
    pallas_call x1, Pallas kernels, local(): pl.pallas_call(functools.partial(exchange_kernel, nodes, most), out_shape...  59.9 us
    pallas_call x1, Pallas kernels, local(): pl.pallas_call(functools.partial(compact_kernel, nodes, most), out_shape=...  17.1 us
    pallas_call x1, Pallas kernels, local(): pl.pallas_call(functools.partial(place_kernel, nodes, most), out_shape=ja...  4.47 us

profile of v1, /device:TPU:15, one launch (start us, length us, event | category | flops | bytes accessed | tf_op | source)
XLA Modules:
  0.0 82.1 jit_solution(11678693098004163012)
XLA Ops:
  0.0 0.6 broadcast_in_dim.3.empty
  0.6 17.1 %compact.1 = (f32[3080,128]{1,0:T(8,128)}, f32[512,128]{1,0:T(8,128)}, s32[3200]{0:T(1024)}, f32[8,128]{1,0:T(8,128)}) custom-call(f32[4096,128]{1,0:T(8,128)} %rows.1, s32[32,128]{1,0:T(8,128)} %bitcast.3, s32[32,128]{1,0:T(8,128)} %bitcast.4, s32[3200]{0:T(1024)} %broadcast_in_dim.3.empty), custom_call_target="tpu_custom_call" | custom-call | tf_op jit(solution)/shard_map/compact/pallas_call | solution.py:239
  17.7 59.9 %exchange.1 = (f32[16,192,128]{2,1,0:T(8,128)}, f32[16,8,128]{2,1,0:T(8,128)}) custom-call(f32[3080,128]{1,0:T(8,128)} %get-tuple-element.11.packed, f32[512,128]{1,0:T(8,128)} %get-tuple-element.12.tail, s32[3200]{0:T(1024)} %get-tuple-element.13.source, f32[8,128]{1,0:T(8,128)} %get-tuple-element.14.counts, f32[1,128]{1,0:T(1,128)} %bitcast.5), custom_call_target="tpu_custom_call" | custom-call | tf_op jit(solution)/shard_map/exchange/pallas_call | solution.py:259
  77.6 4.5 %place.1 = f32[3072,128]{1,0:T(8,128)} custom-call(f32[16,192,128]{2,1,0:T(8,128)} %get-tuple-element.15.got, f32[16,8,128]{2,1,0:T(8,128)} %get-tuple-element.16.gotc), custom_call_target="tpu_custom_call" | custom-call | tf_op jit(solution)/shard_map/place/pallas_call | solution.py:280

commit v2 on v1

--- a/solution.py
+++ b/solution.py
@@ -25,13 +25,10 @@
     return jnp.dot(a, b, preferred_element_type=f32)
 
 
-def compact_kernel(nodes, most, rows, mask, key, empty, packed, tail, source, counts,
-                   place_v, slot_v, place_s, slot_s, sems):
+def compact_kernel(nodes, most, rows, mask, key, packed, tail, source, counts,
+                   running_v, within_v, piece_v, column_v, value_v, running_s, sem):
     lines = mask.shape[0]
     slots = nodes * most
-    fill = pltpu.make_async_copy(empty, source, sems.at[0])
-    fill.start()
-    one = jnp.ones((), f32)
     upper = (iota((LANES, LANES), 0) <= iota((LANES, LANES), 1)).astype(f32).astype(bf16)
     both = jnp.concatenate([upper, jnp.ones((LANES, LANES), bf16)], axis=0)
     group = min(nodes, 16)
@@ -48,46 +45,73 @@
         above = dot(lower, hits).astype(bf16)
         return dot(jnp.concatenate([hits, above], axis=1), both)
 
-    place_v[...] = (prefix(livef, earlier[:lines, :lines]) - livef).astype(i32)
-    slot = (one - livef) * slots
+    running = prefix(livef, earlier[:lines, :lines])
+    running_v[...] = running.astype(i32)
+    fetch = pltpu.make_async_copy(running_v, running_s, sem)
+    fetch.start()
+    within = dot(livef.astype(bf16), upper).astype(i32) - 1
+    within_v[...] = jnp.where(live, within, -1)
+    slot = jnp.zeros((lines, LANES), f32)
     lane = iota((8, LANES), 1)
     parts = []
     for first in range(0, nodes, group):
         hits = [(live & (keys == b)).astype(f32) for b in range(first, first + group)]
-        running = prefix(jnp.concatenate(hits, axis=0), earlier)
+        ranks = prefix(jnp.concatenate(hits, axis=0), earlier)
         for j, hit in enumerate(hits):
             b = first + j
-            mine = running[j * lines:(j + 1) * lines]
+            mine = ranks[j * lines:(j + 1) * lines]
             slot = slot + hit * (mine + (b * most - 1.0))
             parts.append(jnp.where(lane == b % LANES, mine[lines - 1:lines, LANES - 1:LANES], 0.0))
     counts[...] = sum(parts)
-    slot_v[...] = slot.astype(i32)
-    c1 = pltpu.make_async_copy(place_v, place_s, sems.at[1])
-    c2 = pltpu.make_async_copy(slot_v, slot_s, sems.at[2])
-    c1.start()
-    c2.start()
-    fill.wait()
-    c1.wait()
-    c2.wait()
-
-    def line(i, carry):
-        def some(q, carry):
-            for u in range(16):
-                j = q * 16 + u
-                g = place_s[i, j]
-                packed[pl.ds(g, 1), :] = rows[pl.ds(i * LANES + j, 1), :]
-                source[slot_s[i, j]] = g
-            return carry
-        return lax.fori_loop(0, LANES // 16, some, carry)
-
-    lax.fori_loop(0, lines, line, 0)
-    count = place_s[lines - 1, LANES - 1] + (slot_s[lines - 1, LANES - 1] < slots).astype(i32)
+    slot = slot.astype(i32)
+    piece_v[...] = jnp.where(live, slot // LANES, -1)
+    column_v[...] = slot % LANES
+    value_v[...] = slots + 1 - running.astype(i32)
+
+    pieces = slots // LANES
+    down = iota((LANES, LANES), 0)
+    piece_down = iota((pieces, LANES), 0)
+    each = 4
+
+    def invert(q, total):
+        for u in range(each):
+            at = pl.ds(q * each + u, 1)
+            value = value_v[at, :]
+            hit = piece_down == piece_v[at, :]
+            high = jnp.where(hit, (value // LANES).astype(f32), 0.0)
+            low = jnp.where(hit, (value % LANES).astype(f32), 0.0)
+            left = jnp.concatenate([high, low], axis=0).astype(bf16)
+            right = (down == column_v[at, :]).astype(f32).astype(bf16)
+            total = total + lax.dot_general(
+                left, right, (((1,), (1,)), ((), ())), preferred_element_type=f32)
+        return total
+
+    total = lax.fori_loop(0, lines // each, invert, jnp.zeros((2 * pieces, LANES), f32))
+    source[...] = slots - (total[:pieces] * LANES + total[pieces:]).astype(i32)
+    fetch.wait()
+
+    def pack(q, start):
+        for u in range(each):
+            i = q * each + u
+            pick = (down == within_v[pl.ds(i, 1), :]).astype(f32).astype(bf16)
+            x = rows[pl.ds(pl.multiple_of(i * LANES, LANES), LANES), :]
+            high = x.astype(bf16)
+            rest = x - high.astype(f32)
+            middle = rest.astype(bf16)
+            low = (rest - middle.astype(f32)).astype(bf16)
+            got = dot(pick, jnp.concatenate([high, middle, low], axis=1))
+            packed[pl.ds(start, LANES), :] = (
+                got[:, :LANES] + (got[:, LANES:2 * LANES] + got[:, 2 * LANES:]))
+            start = running_s[i, LANES - 1]
+        return start
+
+    count = lax.fori_loop(0, lines // each, pack, jnp.int32(0))
     tail[...] = packed[pl.ds(count - WINDOW, WINDOW), :]
 
 
-def exchange_kernel(nodes, most, packed, tail, source, counts, gain, got, gotc,
-                    tailbuf, w8, w64, sums, mine, other, send,
-                    tsem, qsem, ssem, rsem, cssem, crsem):
+def exchange_kernel(nodes, most, packed, tail, source, counts, gain, out, gotc,
+                    tailbuf, w8, w64, sums, mine, other, send, got,
+                    tsem, qssem, qrsem, ssem, rsem, cssem, crsem, osem):
     slots = nodes * most
     me, rep = lax.axis_index("tm"), lax.axis_index("rep")
     barrier = pltpu.get_barrier_semaphore()
@@ -139,15 +163,9 @@
         w64[pl.ds(a, STEP), :] = stride_sum(w8, a, STEP, 8)
         return carry
 
-    ones = jnp.ones((8, LANES), f32)
-
     def w512_at(c, carry):
         a = pl.multiple_of(c * LANES, LANES)
-        total = stride_sum(w64, WINDOW + a, LANES, 64)
-        sums[pl.ds(a, LANES), :] = total
-        sq = lax.dot_general(ones, total * total, (((1,), (1,)), ((), ())),
-                             precision=lax.Precision.HIGHEST, preferred_element_type=f32)
-        mine[pl.ds(c, 1), :] = sq[0:1]
+        sums[pl.ds(a, LANES), :] = stride_sum(w64, WINDOW + a, LANES, 64)
         return carry
 
     own = WINDOW // STEP + 1
@@ -164,24 +182,7 @@
     lax.fori_loop(1, own + 1, w64_at, 0)
     lax.fori_loop(0, 5, w512_at, 0)
 
-    swap = pltpu.make_async_remote_copy(
-        src_ref=mine, dst_ref=other, send_sem=qsem.at[0], recv_sem=qsem.at[1],
-        device_id={"rep": 1 - rep})
-    swap.start()
     sums[pl.ds(slots, 8), :] = jnp.zeros((8, LANES), f32)
-    swap.wait()
-
-    gains = gain[...]
-
-    def scale(c, carry):
-        a = pl.multiple_of(c * LANES, LANES)
-        full = mine[pl.ds(c, 1), :] + other[pl.ds(c, 1), :]
-        inv = lax.rsqrt(full / F + EPS)
-        column = jnp.broadcast_to(inv, (LANES, LANES)).T
-        sums[pl.ds(a, LANES), :] = sums[pl.ds(a, LANES), :] * gains * column
-        return carry
-
-    lax.fori_loop(0, slots // LANES, scale, 0)
 
     def gather(ref, d):
         def some(q, carry):
@@ -196,22 +197,85 @@
             src_ref=send.at[d], dst_ref=got.at[at], send_sem=ssem.at[d], recv_sem=rsem.at[at],
             device_id={"tm": d})
 
-    def send_block(k, carry):
-        d = lax.rem(me + k, nodes)
+    half = nodes // 2
+    near, far = me // half * half, (me // half + 1) % 2 * half
+    seat = me % half
+
+    def send_block(base, k):
+        d = base + (seat + k) % half
         gather(send, d)
         block_copy(d, me).start()
-        return carry
-
-    lax.fori_loop(1, nodes, send_block, 0)
+
+    def swap_copy(s):
+        return pltpu.make_async_remote_copy(
+            src_ref=mine.at[s], dst_ref=other.at[s], send_sem=qssem.at[s], recv_sem=qrsem.at[s],
+            device_id={"rep": 1 - rep})
+
+    def out_copy(s):
+        return pltpu.make_async_copy(got.at[s], out.at[s], osem.at[s])
+
+    def squares(s):
+        x = got[s]
+        mine[s] = jnp.broadcast_to(jnp.sum(x * x, axis=1, keepdims=True), x.shape)
+        swap_copy(s).start()
+
+    gains = gain[...]
+
+    def norm(s):
+        swap_copy(s).wait()
+        got[s] = got[s] * gains * lax.rsqrt((mine[s] + other[s]) / F + EPS)
+        out_copy(s).start()
+
+    def receive(base, k):
+        s = base + (seat + half - k) % half
+        block_copy(s, s).wait()
+        squares(s)
+        return s
+
+    def loop(first, last, body, carry):
+        return lax.fori_loop(first, last, body, carry)
+
+    def send_far(k, carry):
+        send_block(far, k)
+        return carry
+
+    def send_near(k, carry):
+        send_block(near, k)
+        return carry
+
+    loop(0, half, send_far, 0)
+    loop(1, half, send_near, 0)
     gather(got, me)
+    squares(me)
+
+    def get_far(k, carry):
+        receive(far, k)
+        before = jnp.where(k == 0, me, far + (seat + half - k + 1) % half)
+        norm(before)
+        return carry
+
+    def get_near(k, carry):
+        receive(near, k)
+        before = jnp.where(k == 1, far + (seat + 1) % half, near + (seat + half - k + 1) % half)
+        norm(before)
+        return carry
+
+    loop(0, half, get_far, 0)
+    loop(1, half, get_near, 0)
+    norm(near + (seat + 1) % half)
 
     def finish(k, carry):
         s = lax.rem(me + k, nodes)
         count_copy(s, s).wait()
-        block_copy(s, s).wait()
-        return carry
-
-    lax.fori_loop(1, nodes, finish, 0)
+        return carry
+
+    loop(1, nodes, finish, 0)
+
+    def left(s, carry):
+        out_copy(s).wait()
+        return carry
+
+    loop(0, nodes, left, 0)
 
 
 def place_kernel(nodes, most, got, gotc, out):
@@ -235,27 +299,27 @@
     vm = pl.BlockSpec(memory_space=VMEM)
     sm = pl.BlockSpec(memory_space=SMEM)
     hbm = pl.BlockSpec(memory_space=pl.ANY)
-    empty = jnp.full((slots + LANES,), slots, i32)
+    table = pltpu.VMEM((lines, LANES), i32)
     packed, tail, source, counts = pl.pallas_call(
         functools.partial(compact_kernel, nodes, most),
         out_shape=(
-            jax.ShapeDtypeStruct((slots + 8, half), f32),
+            jax.ShapeDtypeStruct((slots + LANES, half), f32),
             jax.ShapeDtypeStruct((WINDOW, half), f32),
-            jax.ShapeDtypeStruct((slots + LANES,), i32),
+            jax.ShapeDtypeStruct((slots // LANES, LANES), i32),
             jax.ShapeDtypeStruct((8, LANES), f32),
         ),
-        in_specs=[vm, vm, vm, hbm],
-        out_specs=(vm, vm, sm, vm),
+        in_specs=[vm, vm, vm],
+        out_specs=(vm, vm, vm, vm),
         scratch_shapes=[
-            pltpu.VMEM((lines, LANES), i32),
-            pltpu.VMEM((lines, LANES), i32),
+            table, table, table, table, table,
             pltpu.SMEM((lines, LANES), i32),
-            pltpu.SMEM((lines, LANES), i32),
-            pltpu.SemaphoreType.DMA((3,)),
+            pltpu.SemaphoreType.DMA,
         ],
         name="compact",
-    )(rows, row_mask.reshape(lines, LANES), key_bucket.reshape(lines, LANES), empty)
+    )(rows, row_mask.reshape(lines, LANES), key_bucket.reshape(lines, LANES))
+    source = source.reshape(slots)
     dma = pltpu.SemaphoreType.DMA
+    blocks = pltpu.VMEM((nodes, most, half), f32)
     got, gotc = pl.pallas_call(
         functools.partial(exchange_kernel, nodes, most),
         out_shape=(
@@ -263,17 +327,15 @@
             jax.ShapeDtypeStruct((nodes, 8, LANES), f32),
         ),
         in_specs=[vm, vm, sm, vm, vm],
-        out_specs=(vm, vm),
+        out_specs=(hbm, vm),
         scratch_shapes=[
             pltpu.VMEM((WINDOW, half), f32),
             pltpu.VMEM((WINDOW + slots, half), f32),
             pltpu.VMEM((WINDOW + slots, half), f32),
             pltpu.VMEM((slots + 8, half), f32),
-            pltpu.VMEM((slots // LANES, LANES), f32),
-            pltpu.VMEM((slots // LANES, LANES), f32),
-            pltpu.VMEM((nodes, most, half), f32),
-            dma((2,)), dma((2,)), dma((nodes,)), dma((nodes,)), dma((nodes,)), dma((nodes,)),
-        ],
+            blocks, blocks, blocks, blocks,
+            dma((2,)),
+        ] + [dma((nodes,))] * 7,
         compiler_params=pltpu.CompilerParams(collective_id=0, has_side_effects=True),
         name="exchange",
     )(packed, tail, source, counts, gain.reshape(1, half))

time: 82.3 us -> 72.8 us (0.88)
  the two profiles are of different devices: /device:TPU:15 before, /device:TPU:0 now
where the time goes in v2:
time: 72.8 us; the launch traced here: 72.6 us
  Pallas kernels  72.6 us (100%)
    pallas_call x1, Pallas kernels, local(): pl.pallas_call(functools.partial(exchange_kernel, nodes, most), out_shape...  60.7 us
    pallas_call x1, Pallas kernels, local(): pl.pallas_call(functools.partial(compact_kernel, nodes, most), out_shape=...  7.41 us
    pallas_call x1, Pallas kernels, local(): pl.pallas_call(functools.partial(place_kernel, nodes, most), out_shape=ja...  4.47 us

profile of v2, /device:TPU:0, one launch (start us, length us, event | category | flops | bytes accessed | tf_op | source)
XLA Modules:
  0.0 72.6 jit_solution(1944199578112921207)
XLA Ops:
  0.0 7.4 %compact.1 = (f32[3200,128]{1,0:T(8,128)}, f32[512,128]{1,0:T(8,128)}, s32[24,128]{1,0:T(8,128)}, f32[8,128]{1,0:T(8,128)}) custom-call(f32[4096,128]{1,0:T(8,128)} %rows.1, s32[32,128]{1,0:T(8,128)} %bitcast.4, s32[32,128]{1,0:T(8,128)} %bitcast.5), custom_call_target="tpu_custom_call" | custom-call | tf_op jit(solution)/shard_map/compact/pallas_call | solution.py:303
  7.4 60.7 %exchange.1 = (f32[16,192,128]{2,1,0:T(8,128)}, f32[16,8,128]{2,1,0:T(8,128)}) custom-call(f32[3200,128]{1,0:T(8,128)} %get-tuple-element.11.packed, f32[512,128]{1,0:T(8,128)} %get-tuple-element.12.tail, s32[3072]{0:T(1024)} %bitcast.6, f32[8,128]{1,0:T(8,128)} %get-tuple-element.14.counts, f32[1,128]{1,0:T(1,128)} %bitcast.7), custom_call_target="tpu_custom_call" | custom-call | tf_op jit(solution)/shard_map/exchange/pallas_call | solution.py:323
  68.1 4.5 %place.1 = f32[3072,128]{1,0:T(8,128)} custom-call(f32[16,192,128]{2,1,0:T(8,128)} %get-tuple-element.15.got, f32[16,8,128]{2,1,0:T(8,128)} %get-tuple-element.16.gotc), custom_call_target="tpu_custom_call" | custom-call | tf_op jit(solution)/shard_map/place/pallas_call | solution.py:342

commit v3 on v2

v3 whole, which is shorter than its diff:
```python
import functools

import jax
import jax.numpy as jnp
from jax import lax
from jax.experimental import pallas as pl
from jax.experimental.pallas import tpu as pltpu
from jax.sharding import PartitionSpec as P

F = 256
WINDOW = 512
EPS = 1e-06
LANES = 128
STEP = 64
VMEM = pltpu.MemorySpace.VMEM
SMEM = pltpu.MemorySpace.SMEM
f32, bf16, i32 = jnp.float32, jnp.bfloat16, jnp.int32


def iota(shape, axis):
    return lax.broadcasted_iota(i32, shape, axis)


def within(x, low, high):
    return jnp.minimum(jnp.maximum(x, low), high)


def dot(a, b):
    return jnp.dot(a, b, preferred_element_type=f32)


def exchange_kernel(nodes, most, wide, rows_hbm, mask, key, gain, out, gotc,
                    rows, packed, tail, tailbuf, w8, w64, sums, mine, other, send, got, counts,
                    order_v, source_v, first_v, second_v, order_s, source_s,
                    lsem, tsem, qssem, qrsem, ssem, rsem, cssem, crsem, osem):
    slots = nodes * most
    lines = mask.shape[0]
    me, rep = lax.axis_index("tm"), lax.axis_index("rep")
    fetch = pltpu.make_async_copy(rows_hbm, rows, lsem.at[0])
    fetch.start()
    barrier = pltpu.get_barrier_semaphore()

    def hello(k, carry):
        pl.semaphore_signal(barrier, inc=1, device_id={"tm": lax.rem(me + k, nodes)})
        return carry

    lax.fori_loop(1, nodes, hello, 0)
    pl.semaphore_signal(barrier, inc=1, device_id={"rep": 1 - rep})

    upper = (iota((LANES, LANES), 0) <= iota((LANES, LANES), 1)).astype(f32).astype(bf16)
    both = jnp.concatenate([upper, jnp.ones((LANES, LANES), bf16)], axis=0)
    group = min(nodes, 16)
    size = group * lines
    r, c = iota((size, size), 0), iota((size, size), 1)
    earlier = ((r // lines == c // lines) & (c < r)).astype(f32).astype(bf16)
    live = mask[...] == 1
    livef = live.astype(f32)
    keys = key[...]

    def prefix(hits, lower):
        hits = hits.astype(bf16)
        above = dot(lower, hits).astype(bf16)
        return dot(jnp.concatenate([hits, above], axis=1), both)

    down = iota((LANES, LANES), 0)
    each = 4

    def invert(pieces, spot, values):
        first_v[...] = jnp.where(live, spot // LANES, -1)
        second_v[...] = spot % LANES
        piece_down = iota((pieces, LANES), 0)

        def some(q, total):
            for u in range(each):
                i = q * each + u
                high, low = values(i)
                hit = piece_down == first_v[pl.ds(i, 1), :]
                left = jnp.concatenate(
                    [jnp.where(hit, high, 0.0), jnp.where(hit, low, 0.0)], axis=0).astype(bf16)
                right = (down == second_v[pl.ds(i, 1), :]).astype(f32).astype(bf16)
                total = total + lax.dot_general(
                    left, right, (((1,), (1,)), ((), ())), preferred_element_type=f32)
            return total

        total = lax.fori_loop(0, lines // each, some, jnp.zeros((2 * pieces, LANES), f32))
        return (total[:pieces] * LANES + total[pieces:]).astype(i32)

    running = prefix(livef, earlier[:lines, :lines])
    place = running.astype(i32) - 1
    pieces = slots // LANES
    lanef = iota((1, LANES), 1).astype(f32)
    order_v[0:pieces, :] = within(invert(
        pieces, place, lambda i: (jnp.asarray(i, i32).astype(f32), lanef)), 0, lines * LANES - 1)
    order_v[pieces:pieces + 8, :] = within(jnp.broadcast_to(
        running[lines - 1:lines, LANES - 1:LANES], (8, LANES)).astype(i32), WINDOW, slots)
    list_copy = pltpu.make_async_copy(order_v, order_s, lsem.at[1])
    list_copy.start()
    list_copy.wait()
    fetch.wait()
    begin = order_s[pieces, 0] - WINDOW

    def take_tail(q, carry):
        for u in range(16):
            j = q * 16 + u
            g = begin + j
            tail[pl.ds(j, 1), :] = rows[pl.ds(order_s[g >> 7, g & (LANES - 1)], 1), :]
        return carry

    lax.fori_loop(0, WINDOW // 16, take_tail, 0)
    pl.semaphore_wait(barrier, nodes)
    ahead = pltpu.make_async_remote_copy(
        src_ref=tail, dst_ref=tailbuf, send_sem=tsem.at[0], recv_sem=tsem.at[1],
        device_id={"tm": lax.rem(me + 1, nodes)})
    ahead.start()

    slot = jnp.zeros((lines, LANES), f32)
    lane = iota((8, LANES), 1)
    parts = []
    for first in range(0, nodes, group):
        hits = [(live & (keys == b)).astype(f32) for b in range(first, first + group)]
        ranks = prefix(jnp.concatenate(hits, axis=0), earlier)
        for j, hit in enumerate(hits):
            b = first + j
            own = ranks[j * lines:(j + 1) * lines]
            slot = slot + hit * (own + (b * wide - 1.0))
            parts.append(jnp.where(lane == b % LANES, own[lines - 1:lines, LANES - 1:LANES], 0.0))
    counts[...] = sum(parts)
    back = slots - place
    packed[0:lines, :] = (back // LANES).astype(f32)
    packed[lines:2 * lines, :] = (back % LANES).astype(f32)
    source_v[...] = within(slots - invert(
        nodes * wide // LANES, slot.astype(i32),
        lambda i: (packed[pl.ds(i, 1), :], packed[pl.ds(lines + i, 1), :])), 0, slots)
    source_copy = pltpu.make_async_copy(source_v, source_s, lsem.at[2])
    source_copy.start()

    def count_copy(d, at):
        return pltpu.make_async_remote_copy(
            src_ref=counts, dst_ref=gotc.at[at], send_sem=cssem.at[d], recv_sem=crsem.at[at],
            device_id={"tm": d})

    def take(i, carry):
        def some(q, carry):
            for u in range(16):
                j = q * 16 + u
                packed[pl.ds(i * LANES + j, 1), :] = rows[pl.ds(order_s[i, j], 1), :]
            return carry
        return lax.fori_loop(0, LANES // 16, some, carry)

    lax.fori_loop(0, pieces, take, 0)

    def eight(x):
        x = x + pltpu.roll(x, 1, 0)
        x = x + pltpu.roll(x, 2, 0)
        x = x + pltpu.roll(x, 4, 0)
        return x[8:]

    def w8_own(c, carry):
        a = pl.multiple_of(c * STEP, STEP)
        w8[pl.ds(WINDOW + a, STEP), :] = eight(packed[pl.ds(a - 8, STEP + 8), :])
        return carry

    def stride_sum(ref, a, rows, stride):
        parts = [ref[pl.ds(a - stride * k, rows), :] for k in range(8)]
        while len(parts) > 1:
            parts = [parts[i] + parts[i + 1] for i in range(0, len(parts), 2)]
        return parts[0]

    def w64_at(c, carry):
        a = pl.multiple_of(c * STEP, STEP)
        w64[pl.ds(a, STEP), :] = stride_sum(w8, a, STEP, 8)
        return carry

    def w512_at(c, carry):
        a = pl.multiple_of(c * LANES, LANES)
        sums[pl.ds(a, LANES), :] = stride_sum(w64, WINDOW + a, LANES, 64)
        return carry

    own = WINDOW // STEP + 1
    last = (WINDOW + slots) // STEP
    lax.fori_loop(1, slots // STEP, w8_own, 0)
    lax.fori_loop(own + 1, last, w64_at, 0)
    lax.fori_loop(5, slots // LANES, w512_at, 0)
    ahead.wait()
    w8[0:STEP, :] = eight(jnp.concatenate([jnp.zeros((8, LANES), f32), tailbuf[0:STEP, :]], axis=0))
    for a in range(STEP, WINDOW, STEP):
        w8[a:a + STEP, :] = eight(tailbuf[a - 8:a + STEP, :])
    w8[WINDOW:WINDOW + STEP, :] = eight(
        jnp.concatenate([tailbuf[WINDOW - 8:WINDOW, :], packed[0:STEP, :]], axis=0))
    lax.fori_loop(1, own + 1, w64_at, 0)
    lax.fori_loop(0, 5, w512_at, 0)

    sums[pl.ds(slots, 8), :] = jnp.zeros((8, LANES), f32)

    def gather(ref, d):
        def some(q, carry):
            for u in range(8):
                j = q * 8 + u
                at = source_s[d * (wide // LANES) + q // (LANES // 8), q % (LANES // 8) * 8 + u]
                ref[d, pl.ds(j, 1), :] = sums[pl.ds(at, 1), :]
            return carry
        lax.fori_loop(0, most // 8, some, 0)

    def block_copy(d, at):
        return pltpu.make_async_remote_copy(
            src_ref=send.at[d], dst_ref=got.at[at], send_sem=ssem.at[d], recv_sem=rsem.at[at],
            device_id={"tm": d})

    half = nodes // 2
    near, far = me // half * half, (me // half + 1) % 2 * half
    seat = me % half

    def send_block(base, k):
        d = base + (seat + k) % half
        gather(send, d)
        block_copy(d, me).start()

    def swap_copy(s):
        return pltpu.make_async_remote_copy(
            src_ref=mine.at[s], dst_ref=other.at[s], send_sem=qssem.at[s], recv_sem=qrsem.at[s],
            device_id={"rep": 1 - rep})

    def out_copy(s):
        return pltpu.make_async_copy(got.at[s], out.at[s], osem.at[s])

    def squares(s):
        x = got[s]
        mine[s] = jnp.broadcast_to(jnp.sum(x * x, axis=1, keepdims=True), x.shape)
        swap_copy(s).start()

    gains = gain[...]

    def norm(s):
        swap_copy(s).wait()
        got[s] = got[s] * gains * lax.rsqrt((mine[s] + other[s]) / F + EPS)
        out_copy(s).start()

    def receive(base, k):
        s = base + (seat + half - k) % half
        block_copy(s, s).wait()
        squares(s)
        return s

    def loop(first, last, body, carry):
        return lax.fori_loop(first, last, body, carry)

    def send_far(k, carry):
        send_block(far, k)
        return carry

    def send_near(k, carry):
        send_block(near, k)
        return carry

    source_copy.wait()
    loop(0, half, send_far, 0)
    loop(1, half, send_near, 0)

    def send_counts(k, carry):
        count_copy(lax.rem(me + k, nodes), me).start()
        return carry

    loop(1, nodes, send_counts, 0)
    gotc[me] = counts[...]
    gather(got, me)
    squares(me)

    def get_far(k, carry):
        receive(far, k)
        before = jnp.where(k == 0, me, far + (seat + half - k + 1) % half)
        norm(before)
        return carry

    def get_near(k, carry):
        receive(near, k)
        before = jnp.where(k == 1, far + (seat + 1) % half, near + (seat + half - k + 1) % half)
        norm(before)
        return carry

    loop(0, half, get_far, 0)
    loop(1, half, get_near, 0)
    norm(near + (seat + 1) % half)

    def finish(k, carry):
        s = lax.rem(me + k, nodes)
        count_copy(s, s).wait()
        return carry

    loop(1, nodes, finish, 0)

    def left(s, carry):
        out_copy(s).wait()
        return carry

    loop(0, nodes, left, 0)


def place_kernel(nodes, most, got, gotc, out):
    me = lax.axis_index("tm")
    out[...] = jnp.zeros_like(out)
    lane = iota((1, LANES), 1)

    def sender(s, start):
        out[pl.ds(start, most), :] = got[s]
        number = jnp.sum(jnp.where(lane == me, gotc[s, 0:1, :], 0.0))
        return start + number.astype(i32)

    lax.fori_loop(0, nodes, sender, jnp.int32(0))


def local(nodes, rows, row_mask, key_bucket, gain):
    size_rows, half = rows.shape
    most = 3 * size_rows // (4 * nodes)
    slots = nodes * most
    lines = size_rows // LANES
    vm = pl.BlockSpec(memory_space=VMEM)
    hbm = pl.BlockSpec(memory_space=pl.ANY)
    wide = -(-most // LANES) * LANES
    dma = pltpu.SemaphoreType.DMA
    blocks = pltpu.VMEM((nodes, most, half), f32)
    edge = pltpu.VMEM((WINDOW, half), f32)
    table = pltpu.VMEM((lines, LANES), i32)
    order, source = (slots // LANES + 8, LANES), (nodes * wide // LANES, LANES)
    got, gotc = pl.pallas_call(
        functools.partial(exchange_kernel, nodes, most, wide),
        out_shape=(
            jax.ShapeDtypeStruct((nodes, most, half), f32),
            jax.ShapeDtypeStruct((nodes, 8, LANES), f32),
        ),
        in_specs=[hbm, vm, vm, vm],
        out_specs=(hbm, vm),
        scratch_shapes=[
            pltpu.VMEM((size_rows, half), f32),
            pltpu.VMEM((slots, half), f32),
            edge, edge,
            pltpu.VMEM((WINDOW + slots, half), f32),
            pltpu.VMEM((WINDOW + slots, half), f32),
            pltpu.VMEM((slots + 8, half), f32),
            blocks, blocks, blocks, blocks,
            pltpu.VMEM((8, LANES), f32),
            pltpu.VMEM(order, i32), pltpu.VMEM(source, i32),
            table, table,
            pltpu.SMEM(order, i32), pltpu.SMEM(source, i32),
            dma((3,)), dma((2,)),
        ] + [dma((nodes,))] * 7,
        compiler_params=pltpu.CompilerParams(collective_id=0, has_side_effects=True),
        name="exchange",
    )(rows, row_mask.reshape(lines, LANES), key_bucket.reshape(lines, LANES), gain.reshape(1, half))
    return pl.pallas_call(
        functools.partial(place_kernel, nodes, most),
        out_shape=jax.ShapeDtypeStruct((slots, half), f32),
        in_specs=[vm, vm],
        out_specs=vm,
        name="place",
    )(got, gotc)


def solution(mesh):
    in_specs = (P("tm", "rep"), P("tm"), P("tm"), P("rep"))
    body = functools.partial(local, mesh.shape["tm"])
    return jax.shard_map(body, mesh=mesh, in_specs=in_specs, out_specs=P("tm", "rep"), check_vma=False)
```

time: 72.8 us -> 71.6 us (0.984)
  the two profiles are of different devices: /device:TPU:0 before, /device:TPU:15 now
where the time goes in v3:
time: 71.6 us; the launch traced here: 70.6 us
  Pallas kernels  70.6 us (99%)
    pallas_call x1, Pallas kernels, local(): pl.pallas_call(functools.partial(exchange_kernel, nodes, most, wide), out...  66.1 us
    pallas_call x1, Pallas kernels, local(): pl.pallas_call(functools.partial(place_kernel, nodes, most), out_shape=ja...  4.47 us

profile of v3, /device:TPU:15, one launch (start us, length us, event | category | flops | bytes accessed | tf_op | source)
XLA Modules:
  0.0 70.6 jit_solution(12196729655580983655)
XLA Ops:
  0.0 66.1 %exchange.1 = (f32[16,192,128]{2,1,0:T(8,128)}, f32[16,8,128]{2,1,0:T(8,128)}) custom-call(f32[4096,128]{1,0:T(8,128)} %rows_hbm.1, s32[32,128]{1,0:T(8,128)} %bitcast.3, s32[32,128]{1,0:T(8,128)} %bitcast.4, f32[1,128]{1,0:T(1,128)} %bitcast.5), custom_call_target="tpu_custom_call" | custom-call | tf_op jit(solution)/shard_map/exchange/pallas_call | solution.py:324
  66.1 4.5 %place.1 = f32[3072,128]{1,0:T(8,128)} custom-call(f32[16,192,128]{2,1,0:T(8,128)} %get-tuple-element.7.got, f32[16,8,128]{2,1,0:T(8,128)} %get-tuple-element.8.gotc), custom_call_target="tpu_custom_call" | custom-call | tf_op jit(solution)/shard_map/place/pallas_call | solution.py:349

commit v4 on v3

--- a/solution.py
+++ b/solution.py
@@ -244,17 +244,14 @@
     def loop(first, last, body, carry):
         return lax.fori_loop(first, last, body, carry)
 
-    def send_far(k, carry):
+    def send_both(k, carry):
         send_block(far, k)
-        return carry
-
-    def send_near(k, carry):
         send_block(near, k)
         return carry
 
     source_copy.wait()
-    loop(0, half, send_far, 0)
-    loop(1, half, send_near, 0)
+    send_block(far, 0)
+    loop(1, half, send_both, 0)
 
     def send_counts(k, carry):
         count_copy(lax.rem(me + k, nodes), me).start()
@@ -265,20 +262,16 @@
     gather(got, me)
     squares(me)
 
-    def get_far(k, carry):
-        receive(far, k)
-        before = jnp.where(k == 0, me, far + (seat + half - k + 1) % half)
-        norm(before)
-        return carry
-
-    def get_near(k, carry):
+    def get_both(k, carry):
+        s = receive(far, k)
+        norm(jnp.where(k == 1, far + seat, near + (seat + half - k + 1) % half))
         receive(near, k)
-        before = jnp.where(k == 1, far + (seat + 1) % half, near + (seat + half - k + 1) % half)
-        norm(before)
-        return carry
-
-    loop(0, half, get_far, 0)
-    loop(1, half, get_near, 0)
+        norm(s)
+        return carry
+
+    receive(far, 0)
+    norm(me)
+    loop(1, half, get_both, 0)
     norm(near + (seat + 1) % half)
 
     def finish(k, carry):
@@ -295,17 +288,33 @@
     loop(0, nodes, left, 0)
 
 
-def place_kernel(nodes, most, got, gotc, out):
+def place_kernel(nodes, most, got_hbm, gotc, out, got, starts_v, starts_s, gsem, sem):
     me = lax.axis_index("tm")
+
+    def block(s):
+        return pltpu.make_async_copy(got_hbm.at[s], got.at[s], gsem.at[s])
+
+    def begin(s, carry):
+        block(s).start()
+        return carry
+
+    lax.fori_loop(0, nodes, begin, 0)
+    shape = (nodes, nodes * 8)
+    before = (iota(shape, 1) % 8 == 0) & (iota(shape, 1) // 8 < iota(shape, 0))
+    numbers = gotc[...].reshape(nodes * 8, LANES).astype(bf16)
+    starts = dot(before.astype(f32).astype(bf16), numbers).astype(i32)
+    starts_v[...] = within(starts, 0, (nodes - 1) * most)
+    fetch = pltpu.make_async_copy(starts_v, starts_s, sem)
+    fetch.start()
     out[...] = jnp.zeros_like(out)
-    lane = iota((1, LANES), 1)
-
-    def sender(s, start):
-        out[pl.ds(start, most), :] = got[s]
-        number = jnp.sum(jnp.where(lane == me, gotc[s, 0:1, :], 0.0))
-        return start + number.astype(i32)
-
-    lax.fori_loop(0, nodes, sender, jnp.int32(0))
+    fetch.wait()
+
+    def sender(s, carry):
+        block(s).wait()
+        out[pl.ds(starts_s[s, me], most), :] = got[s]
+        return carry
+
+    lax.fori_loop(0, nodes, sender, 0)
 
 
 def local(nodes, rows, row_mask, key_bucket, gain):
@@ -349,8 +358,13 @@
     return pl.pallas_call(
         functools.partial(place_kernel, nodes, most),
         out_shape=jax.ShapeDtypeStruct((slots, half), f32),
-        in_specs=[vm, vm],
+        in_specs=[hbm, vm],
         out_specs=vm,
+        scratch_shapes=[
+            blocks,
+            pltpu.VMEM((nodes, LANES), i32), pltpu.SMEM((nodes, LANES), i32),
+            dma((nodes,)), dma,
+        ],
         name="place",
     )(got, gotc)
 

time: 71.6 us -> 69.5 us (0.971)
  the two profiles are of different devices: /device:TPU:15 before, /device:TPU:21 now
where the time goes in v4:
time: 69.5 us; the launch traced here: 69.2 us
  Pallas kernels  69.2 us (100%)
    pallas_call x1, Pallas kernels, local(): pl.pallas_call(functools.partial(exchange_kernel, nodes, most, wide), out...  65.6 us
    pallas_call x1, Pallas kernels, local(): pl.pallas_call(functools.partial(place_kernel, nodes, most), out_shape=ja...  3.59 us

profile of v4, /device:TPU:21, one launch (start us, length us, event | category | flops | bytes accessed | tf_op | source)
XLA Modules:
  0.0 69.2 jit_solution(14433237359234328261)
XLA Ops:
  0.0 65.6 %exchange.1 = (f32[16,192,128]{2,1,0:T(8,128)}, f32[16,8,128]{2,1,0:T(8,128)}) custom-call(f32[4096,128]{1,0:T(8,128)} %rows_hbm.1, s32[32,128]{1,0:T(8,128)} %bitcast.3, s32[32,128]{1,0:T(8,128)} %bitcast.4, f32[1,128]{1,0:T(1,128)} %bitcast.5), custom_call_target="tpu_custom_call" | custom-call | tf_op jit(solution)/shard_map/exchange/pallas_call | solution.py:333
  65.6 3.6 %place.1 = f32[3072,128]{1,0:T(8,128)} custom-call(f32[16,192,128]{2,1,0:T(8,128)} %get-tuple-element.7.got_hbm, f32[16,8,128]{2,1,0:T(8,128)} %get-tuple-element.8.gotc), custom_call_target="tpu_custom_call" | custom-call | tf_op jit(solution)/shard_map/place/pallas_call | solution.py:358
